TPU v7x, 32 devices: a whole 2x2x4 slice. The times are simulated.
32 devices in a mesh: section: 2 (over core), ctx: 8 (over z, x), dp: 2 (over y).
Axes of the slice: x: 2, y: 2, z: 4, core: 2. Of those that a mesh axis runs over, the one named last changes fastest.
Arguments:
- hidden: bfloat16 [4, 2048, 5376], P(('section', 'dp'), 'ctx'), may hold values from -6 to 6
- frozen_query_rows: bfloat16 [4, 2048, 2048], P(('section', 'dp'), 'ctx'), may hold values from -12 to 12
- frozen_key_rows: bfloat16 [4, 2048, 1024], P(('section', 'dp'), 'ctx'), may hold values from -12 to 12
- frozen_value_rows: bfloat16 [4, 2048, 1024], P(('section', 'dp'), 'ctx'), may hold values from -6 to 6
- next_output_gradient: bfloat16 [4, 2048, 2048], P(('section', 'dp'), 'ctx'), may hold values from -0.011962891 to 0.011962891
- document_lengths: int32 [4, 16], P(('section', 'dp')), may hold values from 1 to 512, 2048 in all within a row
- document_adapter: int32 [4, 16], P(('section', 'dp')), may hold values from 0 to 3
- adapter_down_maps: bfloat16 [5376, 2, 4, 16], replicated, may hold values from -0.078125 to 0.078125
- adapter_up_maps: bfloat16 [2, 4, 16, 1024], replicated, may hold values from -1.5 to 1.5
Outputs:
- handed_on: bfloat16 [4, 2048, 2048], P(('section', 'dp'), 'ctx')
- down_map_gradient: float32 [5376, 2, 4, 16], replicated
- up_map_gradient: float32 [2, 4, 16, 1024], replicated
Inputs may be any that keep to these rules, and one draw needn't show every extreme that they name: `document_lengths`: each sequence's 16 lengths sum to 2048, and the longest is exactly 512.
All inputs are finite; a program needn't handle non-finite values.
Results may differ from a plain program's by a relative error of at most 0.016.
Values may be sent and summed in bfloat16 or wider, within the bound.
No kernel may reach another device: no remote copies, remote signals or barrier semaphores. Data moves between devices by JAX's collectives and lax.ppermute only.
A program may use at most 128 MiB of HBM per device.

v0:
```python
from functools import partial
import jax
import jax.numpy as jnp
from jax import lax
from jax.sharding import PartitionSpec as P

HD = 128
WINDOW = 1024
query_scale = 168.0 ** (-0.5)
adapter_scale = 0.5
rope_base = 10000.0
masked_score = -1e30


def passed_along(value, axis, by):
    length = lax.axis_size(axis)
    return lax.ppermute(value, axis, [(i, (i + by) % length) for i in range(length)])


def passed_along_2(value, axis, steps):
    count = lax.axis_size(axis)
    initial, last = (max(0, -steps), min(count, count - steps))
    return lax.ppermute(value, axis, [(source, source + steps) for source in range(initial, last)])


def rotate(vectors, positions, direction):
    head_dim = vectors.shape[-1]
    half_dim = head_dim // 2
    frequency = rope_base ** (-(jnp.arange(half_dim, dtype=jnp.float32) * 2.0) / head_dim)
    angles = positions[:, None] * frequency[None, :]
    cos_part = jnp.cos(angles)[:, None, :]
    sine_part = direction * jnp.sin(angles)[:, None, :]
    front_half = vectors[..., :half_dim]
    back_half = vectors[..., half_dim:]
    return jnp.concatenate(
        [
            front_half * cos_part - back_half * sine_part,
            back_half * cos_part + front_half * sine_part,
        ],
        axis=-1,
    )


def doc_index(sequence_lengths, positions):
    doc_ends = jnp.cumsum(sequence_lengths)
    return jnp.sum((doc_ends[None, :] <= positions[:, None]).astype(jnp.int32), axis=1)


def tenant_rows(sequence_lengths, adapter_bank, positions):
    doc_ids = doc_index(sequence_lengths, positions)
    picked = (
        doc_ids[:, None] == jnp.arange(sequence_lengths.shape[0], dtype=jnp.int32)[None, :]
    ).astype(jnp.int32)
    return (doc_ids, jnp.sum(picked * adapter_bank[None, :], axis=1))


def adapter_token_rows(
    hidden, frozen_key_rows, frozen_value_rows, adapter_down_maps, adapter_up_maps, adapter_choice
):
    token_row_count = hidden.shape[0]
    adapter_choices = adapter_up_maps.shape[1]
    adapter_rank_size = adapter_up_maps.shape[2]
    key_value_width = adapter_up_maps.shape[3]
    adapter_onehot_mask = (
        adapter_choice[:, None] == jnp.arange(adapter_choices, dtype=jnp.int32)[None, :]
    ).astype(jnp.float32)
    low_rank_rows = jnp.dot(
        hidden,
        adapter_down_maps.reshape(
            adapter_down_maps.shape[0], 2 * adapter_choices * adapter_rank_size
        ),
        preferred_element_type=jnp.float32,
    )
    low_rank_rows = low_rank_rows.reshape(token_row_count, 2, adapter_choices, adapter_rank_size)
    low_rank = jnp.sum(low_rank_rows * adapter_onehot_mask[:, None, :, None], axis=2).astype(
        jnp.bfloat16
    )
    adapter_spread = low_rank[:, :, None, :] * adapter_onehot_mask[:, None, :, None].astype(
        jnp.bfloat16
    )
    key_adapter_shift = jnp.dot(
        adapter_spread[:, 0].reshape(token_row_count, adapter_choices * adapter_rank_size),
        adapter_up_maps[0].reshape(adapter_choices * adapter_rank_size, key_value_width),
        preferred_element_type=jnp.float32,
    )
    value_adapter_shift = jnp.dot(
        adapter_spread[:, 1].reshape(token_row_count, adapter_choices * adapter_rank_size),
        adapter_up_maps[1].reshape(adapter_choices * adapter_rank_size, key_value_width),
        preferred_element_type=jnp.float32,
    )
    key_before_rotary = frozen_key_rows.astype(jnp.float32) + adapter_scale * key_adapter_shift
    value_token_rows = (
        frozen_value_rows.astype(jnp.float32) + adapter_scale * value_adapter_shift
    ).astype(jnp.bfloat16)
    return (adapter_onehot_mask, adapter_spread, key_before_rotary, value_token_rows)


def adapter_gradients(
    hidden, adapter_spread, adapter_onehot_mask, key_gradient, value_gradient, adapter_up_maps
):
    token_row_count = hidden.shape[0]
    adapter_choices = adapter_up_maps.shape[1]
    adapter_rank_size = adapter_up_maps.shape[2]
    key_value_width = adapter_up_maps.shape[3]
    up_gradient_parts = []
    down_parts = []
    for adapter_selector, adapter_field_gradient in ((0, key_gradient), (1, value_gradient)):
        flat_adapter_spread = adapter_spread[:, adapter_selector].reshape(
            token_row_count, adapter_choices * adapter_rank_size
        )
        up_gradient_parts.append(
            adapter_scale
            * jnp.dot(
                flat_adapter_spread.T, adapter_field_gradient, preferred_element_type=jnp.float32
            )
        )
        low_rank_gradient = adapter_scale * jnp.dot(
            adapter_field_gradient,
            adapter_up_maps[adapter_selector]
            .reshape(adapter_choices * adapter_rank_size, key_value_width)
            .T,
            preferred_element_type=jnp.float32,
        )
        down_parts.append(
            (
                low_rank_gradient.reshape(token_row_count, adapter_choices, adapter_rank_size)
                * adapter_onehot_mask[:, :, None]
            ).astype(jnp.bfloat16)
        )
    up_map_gradient = jnp.stack(up_gradient_parts).reshape(
        2, adapter_choices, adapter_rank_size, key_value_width
    )
    low_grads = jnp.stack(down_parts, axis=1).reshape(
        token_row_count, 2 * adapter_choices * adapter_rank_size
    )
    down_map_gradient = jnp.dot(hidden.T, low_grads, preferred_element_type=jnp.float32).reshape(
        hidden.shape[1], 2, adapter_choices, adapter_rank_size
    )
    return (down_map_gradient, up_map_gradient)


def masked_scores(query_part, key_part, allowed):
    scores = (
        jnp.einsum("trd,ld->trl", query_part, key_part, preferred_element_type=jnp.float32)
        * query_scale
    )
    return jnp.where(allowed[:, None, :], scores, masked_score)


def group_forward(operands, allowed):
    query_part, key_part, value_part = operands
    scores = masked_scores(query_part, key_part, allowed)
    row_max = jnp.max(scores, axis=2, keepdims=True)
    shifted = jnp.exp(scores - row_max)
    row_total = jnp.sum(shifted, axis=2, keepdims=True)
    weights = (shifted / row_total).astype(jnp.bfloat16)
    output_rows = jnp.einsum(
        "trl,ld->trd", weights, value_part, preferred_element_type=jnp.float32
    ).astype(jnp.bfloat16)
    return (output_rows, (row_max + jnp.log(row_total))[..., 0])


def group_backward(operands, allowed):
    query_part, key_part, value_part, out_part, grad_part, log_total = operands
    scores = masked_scores(query_part, key_part, allowed)
    weights = jnp.exp(scores - log_total[:, :, None])
    weights_low = weights.astype(jnp.bfloat16)
    drift_rows = jnp.sum(grad_part.astype(jnp.float32) * out_part.astype(jnp.float32), axis=2)
    grad_weights = jnp.einsum(
        "trd,ld->trl", grad_part, value_part, preferred_element_type=jnp.float32
    )
    grad_scores = (weights * (grad_weights - drift_rows[:, :, None])).astype(jnp.bfloat16)
    value_step = jnp.einsum(
        "trl,trd->ld", weights_low, grad_part, preferred_element_type=jnp.float32
    )
    key_step = (
        jnp.einsum("trl,trd->ld", grad_scores, query_part, preferred_element_type=jnp.float32)
        * query_scale
    )
    return (key_step, value_step)


def body(
    hidden,
    frozen_query_rows,
    frozen_key_rows,
    frozen_value_rows,
    next_output_gradient,
    document_lengths,
    document_adapter,
    adapter_down_maps,
    adapter_up_maps,
):
    tok_rows = hidden.shape[1]
    query_width = frozen_query_rows.shape[2]
    key_value_width = frozen_key_rows.shape[2]
    kv_heads = key_value_width // HD
    group_size = query_width // key_value_width
    ctx_index = lax.axis_index("ctx")
    reach_devs = min(WINDOW // tok_rows, lax.axis_size("ctx") - 1)
    returned_values = passed_along(next_output_gradient, "section", -1)
    positions = ctx_index * tok_rows + jnp.arange(tok_rows, dtype=jnp.int32)
    doc_ids, adapter_choice = tenant_rows(document_lengths[0], document_adapter[0], positions)
    adapter_onehot_mask, adapter_spread, key_before_rotary, value_token_rows = adapter_token_rows(
        hidden[0],
        frozen_key_rows[0],
        frozen_value_rows[0],
        adapter_down_maps,
        adapter_up_maps,
        adapter_choice,
    )
    pos_float = positions.astype(jnp.float32)
    key_rows = (
        rotate(key_before_rotary.reshape(tok_rows, kv_heads, HD), pos_float, 1.0)
        .astype(jnp.bfloat16)
        .reshape(tok_rows, key_value_width)
    )
    query_rows = rotate(
        frozen_query_rows[0].astype(jnp.float32).reshape(tok_rows, kv_heads * group_size, HD),
        pos_float,
        1.0,
    ).astype(jnp.bfloat16)
    received = []
    moving = (key_rows, value_token_rows)
    for distance in range(reach_devs):
        moving = passed_along_2((moving[0], moving[1]), "ctx", 1)
        received.append(moving)
    far_first = received[::-1]
    key_all = jnp.concatenate([kv_pair[0] for kv_pair in far_first] + [key_rows], axis=0)
    value_all = jnp.concatenate([kv_pair[1] for kv_pair in far_first] + [value_token_rows], axis=0)
    key_pos = (ctx_index - reach_devs) * tok_rows + jnp.arange(
        (reach_devs + 1) * tok_rows, dtype=jnp.int32
    )
    key_docs = doc_index(document_lengths[0], key_pos)
    key_gap = positions[:, None] - key_pos[None, :]
    allowed = (
        (doc_ids[:, None] == key_docs[None, :])
        & (key_gap >= 0)
        & (key_gap < WINDOW)
        & (key_pos >= 0)[None, :]
    )
    query_groups = jnp.moveaxis(query_rows.reshape(tok_rows, kv_heads, group_size, HD), 1, 0)
    key_groups = jnp.moveaxis(key_all.reshape(-1, kv_heads, HD), 1, 0)
    value_groups = jnp.moveaxis(value_all.reshape(-1, kv_heads, HD), 1, 0)
    out_groups, log_groups = lax.map(
        partial(group_forward, allowed=allowed), (query_groups, key_groups, value_groups)
    )
    attention_output = jnp.moveaxis(out_groups, 0, 1).reshape(1, tok_rows, query_width)
    handed = passed_along(attention_output, "section", 1)
    grad_groups = jnp.moveaxis(returned_values[0].reshape(tok_rows, kv_heads, group_size, HD), 1, 0)
    key_grads, value_grads = lax.map(
        partial(group_backward, allowed=allowed),
        (query_groups, key_groups, value_groups, out_groups, grad_groups, log_groups),
    )
    key_grads = jnp.moveaxis(key_grads, 0, 1).reshape(-1, key_value_width)
    value_grads = jnp.moveaxis(value_grads, 0, 1).reshape(-1, key_value_width)

    def rows_at(field_rows, distance):
        return field_rows[
            (reach_devs - distance) * tok_rows : (reach_devs - distance + 1) * tok_rows
        ]

    carried = (rows_at(key_grads, reach_devs), rows_at(value_grads, reach_devs))
    for distance in range(reach_devs - 1, -1, -1):
        carried = passed_along_2((carried[0], carried[1]), "ctx", -1)
        carried = (
            carried[0] + rows_at(key_grads, distance),
            carried[1] + rows_at(value_grads, distance),
        )
    key_back, value_back = carried
    key_gradient = (
        rotate(key_back.reshape(tok_rows, kv_heads, HD), pos_float, -1.0)
        .astype(jnp.bfloat16)
        .reshape(tok_rows, key_value_width)
    )
    value_gradient = value_back.astype(jnp.bfloat16)
    down_map_gradient, up_map_gradient = adapter_gradients(
        hidden[0],
        adapter_spread,
        adapter_onehot_mask,
        key_gradient,
        value_gradient,
        adapter_up_maps,
    )
    summed = lax.psum((down_map_gradient, up_map_gradient), ("section", "ctx", "dp"))
    return (handed, summed[0], summed[1])


def solution(mesh):
    return jax.shard_map(
        body,
        mesh=mesh,
        in_specs=(
            P(("section", "dp"), "ctx", None),
            P(("section", "dp"), "ctx", None),
            P(("section", "dp"), "ctx", None),
            P(("section", "dp"), "ctx", None),
            P(("section", "dp"), "ctx", None),
            P(("section", "dp"), None),
            P(("section", "dp"), None),
            P(),
            P(),
        ),
        out_specs=(P(("section", "dp"), "ctx", None), P(), P()),
        check_vma=False,
    )
```

profile of v0, /device:TPU:0, one launch (start us, length us, event | category | flops | bytes accessed | tf_op | source)
XLA Modules:
  0.0 638.7 jit_solution(13565225289575519029)
XLA Ops:
  17.9 5.7 collective-permute-start
  24.7 3.5 collective-permute-start.4
  28.1 6.9 %collective-permute-done = bf16[256,1024]{0,1:T(8,128)(2,1)} collective-permute-done((bf16[256,1024]{0,1:T(8,128)(2,1)S(1)}, bf16[256,1024]{0,1:T(8,128)(2,1)}, u32[]{:S(2)}, u32[]{:S(2)}) %collective-permute-start) | collective-permute-done | bytes 524320 | tf_op jit(solution)/shard_map/ppermute | solution.py:23
  35.0 5.3 collective-permute-start.1
  46.4 5.2 collective-permute-start.5
  51.5 6.1 collective-permute-done.1
  57.6 5.2 collective-permute-start.2
  68.8 5.2 collective-permute-start.6
  74.0 6.0 collective-permute-done.2
  80.1 4.4 collective-permute-start.3
  87.5 3.8 collective-permute-done.6
  91.3 5.2 collective-permute-start.7
  96.5 6.1 collective-permute-done.3
  109.8 4.4 copy.48
  121.6 46.0 %while.26 = (s32[]{:T(128)}, bf16[8,256,2,128]{3,1,2,0:T(8,128)(2,1)}, f32[8,256,2]{1,2,0:T(2,128)}, bf16[8,256,2,128]{3,1,2,0:T(8,128)(2,1)}, bf16[8,1280,128]{...) while((s32[]{:T(128)}, ...), condition=%wide.region_8.9_spmd.clone, body=%wide.region_5.8_spmd.clone.sunk | while | flops 343145984 | bytes 9469813 | solution.py:245
  167.7 127.0 %while.27 = (s32[]{:T(128)}, f32[8,1280,128]{1,2,0:T(8,128)}, f32[8,1280,128]{1,2,0:T(8,128)}, bf16[8,256,2,128]{3,1,2,0:T(8,128)(2,1)}, bf16[8,1280,128]{2,1,0:...) while((s32[]{:T(128)}, f32[8,1280,128]{1,2,0:T(8,128)}, ...), condition=%wide.region_11.12_spmd.clone, body=%wide.region_9.11_spmd.clone.sunk | while | flops 678395392 | bytes 14472769 | solution.py:251
  168.9 3.3 fusion.128
  174.3 3.9 fusion.130
  184.8 3.3 fusion.128
  190.2 3.9 fusion.130
  200.6 3.3 fusion.128
  206.1 3.9 fusion.130
  212.2 3.1 fusion.131
  216.6 3.3 fusion.128
  222.0 3.9 fusion.130
  228.1 3.1 fusion.131
  232.5 3.3 fusion.128
  238.0 3.9 fusion.130
  244.1 3.0 fusion.131
  248.3 3.3 fusion.128
  253.8 3.9 fusion.130
  259.9 3.0 fusion.131
  264.2 3.3 fusion.128
  269.7 3.9 fusion.130
  280.1 3.3 fusion.128
  285.5 3.9 fusion.130
  301.2 24.9 %collective-permute-done.14 = f32[256,1024]{0,1:T(8,128)S(1)} collective-permute-done((f32[256,1024]{0,1:T(8,128)S(1)}, f32[256,1024]{0,1:T(8,128)S(1)}, u32[]{:S(2)}, u32[]{:S(2)}) %collective-permute-start.14) | collective-permute-done | bytes 1048608 | tf_op jit(solution)/shard_map/ppermute | solution.py:23
  327.6 21.0 %collective-permute-done.10 = f32[256,1024]{0,1:T(8,128)S(1)} collective-permute-done((f32[256,1024]{0,1:T(8,128)S(1)}, f32[256,1024]{0,1:T(8,128)S(1)}, u32[]{:S(2)}, u32[]{:S(2)}) %collective-permute-start.10) | collective-permute-done | bytes 1048608 | tf_op jit(solution)/shard_map/ppermute | solution.py:23
  350.1 21.0 %collective-permute-done.15 = f32[256,1024]{0,1:T(8,128)S(1)} collective-permute-done((f32[256,1024]{0,1:T(8,128)S(1)}, f32[256,1024]{0,1:T(8,128)S(1)}, u32[]{:S(2)}, u32[]{:S(2)}) %collective-permute-start.15) | collective-permute-done | bytes 1048608 | tf_op jit(solution)/shard_map/ppermute | solution.py:23
  372.6 21.0 %collective-permute-done.11 = f32[256,1024]{0,1:T(8,128)S(1)} collective-permute-done((f32[256,1024]{0,1:T(8,128)S(1)}, f32[256,1024]{0,1:T(8,128)S(1)}, u32[]{:S(2)}, u32[]{:S(2)}) %collective-permute-start.11) | collective-permute-done | bytes 1048608 | tf_op jit(solution)/shard_map/ppermute | solution.py:23
  395.0 21.0 %collective-permute-done.16 = f32[256,1024]{0,1:T(8,128)S(1)} collective-permute-done((f32[256,1024]{0,1:T(8,128)S(1)}, f32[256,1024]{0,1:T(8,128)S(1)}, u32[]{:S(2)}, u32[]{:S(2)}) %collective-permute-start.16) | collective-permute-done | bytes 1048608 | tf_op jit(solution)/shard_map/ppermute | solution.py:23
  417.5 21.0 %collective-permute-done.12 = f32[256,1024]{0,1:T(8,128)S(1)} collective-permute-done((f32[256,1024]{0,1:T(8,128)S(1)}, f32[256,1024]{0,1:T(8,128)S(1)}, u32[]{:S(2)}, u32[]{:S(2)}) %collective-permute-start.12) | collective-permute-done | bytes 1048608 | tf_op jit(solution)/shard_map/ppermute | solution.py:23
  440.3 20.8 %collective-permute-done.17 = f32[256,1024]{0,1:T(8,128)S(1)} collective-permute-done((f32[256,1024]{0,1:T(8,128)S(1)}, f32[256,1024]{0,1:T(8,128)S(1)}, u32[]{:S(2)}, u32[]{:S(2)}) %collective-permute-start.17) | collective-permute-done | bytes 1048608 | tf_op jit(solution)/shard_map/ppermute | solution.py:23
  461.7 18.9 %collective-permute-done.13 = f32[256,1024]{0,1:T(8,128)S(1)} collective-permute-done((f32[256,1024]{0,1:T(8,128)S(1)}, f32[256,1024]{0,1:T(8,128)S(1)}, u32[]{:S(2)}, u32[]{:S(2)}) %collective-permute-start.13) | collective-permute-done | bytes 1048608 | tf_op jit(solution)/shard_map/ppermute | solution.py:23
  484.5 3.3 copy.49
  490.4 3.3 collective-permute-done.8
  493.7 131.4 %all-reduce.3.cloned.1.call-done = (f32[5376,2,4,16]{0,3,2,1:T(8,128)}, f32[2,4,16,1024]{3,2,1,0:T(8,128)}) async-done(((f32[5376,2,4,16]{0,3,2,1:T(8,128)}, f32[2,4,16,1024]{3,2,1,0:T(8,128)}), (f32[5376,2,4,16]{0,3,2,1:T(8,128)}, f32[2,4,16,1024]{3,2,1,0:T(8,128)})) %all-reduce.3.cloned.1.call-update) | async-done | bytes 3276816 | tf_op jit(solution)/shard_map/psum | solution.py:285
  627.5 3.6 copy.114
  (319 shorter events, 169.1 us)
Async XLA Ops:
  7.2 618.0 %all-reduce.3.cloned.1.call-start = ((), (), s32[]{:S(2)}) async-start(), calls=%async_computation | async-start | bytes 6553600 | tf_op jit(solution)/shard_map/psum | solution.py:285
  15.5 8.0 %copy-start.5 = (bf16[2,4,16,1024]{3,2,1,0:T(8,128)(2,1)S(1)}, bf16[2,4,16,1024]{3,2,1,0:T(8,128)(2,1)}, u32[]{:S(2)}) copy-start(bf16[2,4,16,1024]{3,2,1,0:T(8,128)(2,1)} %param.21) | copy-start | bytes 786436
  15.5 8.0 %copy-start.22 = (bf16[1,256,1024]{2,1,0:T(8,128)(2,1)S(1)}, bf16[1,256,1024]{2,1,0:T(8,128)(2,1)}, u32[]{:S(2)}) copy-start(bf16[1,256,1024]{2,1,0:T(8,128)(2,1)} %param.16) | copy-start | bytes 1572868
  17.9 17.2 %collective-permute-start = (bf16[256,1024]{0,1:T(8,128)(2,1)S(1)}, bf16[256,1024]{0,1:T(8,128)(2,1)}, u32[]{:S(2)}, u32[]{:S(2)}) collective-permute-start(bf16[256,1024]{0,1:T(8,128)(2,1)S(1)} %bitcast.243), channel_id=1, source_target_pairs={{0,2},{2,4},{4,6},{6,8},{8,10},{10,12},{12,14},{1,3},{3,5},{5,7},{... | collective-permute-start | bytes 1572872 | tf_op jit(solution)/shard_map/ppermute | solution.py:23
  24.7 21.7 %collective-permute-start.4 = (bf16[256,1024]{1,0:T(8,128)(2,1)}, bf16[256,1024]{1,0:T(8,128)(2,1)}, u32[]{:S(2)}, u32[]{:S(2)}) collective-permute-start(bf16[256,1024]{1,0:T(8,128)(2,1)} %fusion.59), channel_id=1, source_target_pairs={{0,2},{2,4},{4,6},{6,8},{8,10},{10,12},{12,14},{1,3},{3,5},{5,7},{... | collective-permute-start | bytes 1572872 | tf_op jit(solution)/shard_map/ppermute | solution.py:23
  35.0 22.6 %collective-permute-start.1 = (bf16[256,1024]{0,1:T(8,128)(2,1)}, bf16[256,1024]{0,1:T(8,128)(2,1)}, u32[]{:S(2)}, u32[]{:S(2)}) collective-permute-start(bf16[256,1024]{0,1:T(8,128)(2,1)} %collective-permute-done), channel_id=1, source_target_pairs={{0,2},{2,4},{4,6},{6,8},{8,10},{10,12},{12,14},{1,3},{3,5},{5,7},{... | collective-permute-start | bytes 1572872 | tf_op jit(solution)/shard_map/ppermute | solution.py:23
  42.6 125.1 %collective-permute-start.9 = (bf16[1,256,2048]{1,2,0:T(8,128)(2,1)}, bf16[1,256,2048]{1,2,0:T(8,128)(2,1)}, u32[]{:S(2)}, u32[]{:S(2)}) collective-permute-start(bf16[1,256,2048]{1,2,0:T(8,128)(2,1)} %copy.50), channel_id=1, source_target_pairs={{0,16},{16,0},{1,17},{17,1},{2,18},{18,2},{3,19},{19,3},{4,20},{20... | collective-permute-start | bytes 3145736 | tf_op jit(solution)/shard_map/ppermute | solution.py:17
  46.4 22.5 %collective-permute-start.5 = (bf16[256,1024]{1,0:T(8,128)(2,1)}, bf16[256,1024]{1,0:T(8,128)(2,1)}, u32[]{:S(2)}, u32[]{:S(2)}) collective-permute-start(bf16[256,1024]{1,0:T(8,128)(2,1)} %collective-permute-done.4), channel_id=1, source_target_pairs={{0,2},{2,4},{4,6},{6,8},{8,10},{10,12},{12,14},{1,3},{3,5},{5,7},{... | collective-permute-start | bytes 1572872 | tf_op jit(solution)/shard_map/ppermute | solution.py:23
  57.6 22.5 %collective-permute-start.2 = (bf16[256,1024]{0,1:T(8,128)(2,1)}, bf16[256,1024]{0,1:T(8,128)(2,1)}, u32[]{:S(2)}, u32[]{:S(2)}) collective-permute-start(bf16[256,1024]{0,1:T(8,128)(2,1)} %collective-permute-done.1), channel_id=1, source_target_pairs={{0,2},{2,4},{4,6},{6,8},{8,10},{10,12},{12,14},{1,3},{3,5},{5,7},{... | collective-permute-start | bytes 1572872 | tf_op jit(solution)/shard_map/ppermute | solution.py:23
  66.9 17.6 %copy-start.1 = (f32[256,64]{1,0:T(8,128)S(1)}, f32[256,64]{1,0:T(8,128)}, u32[]{:S(2)}) copy-start(f32[256,64]{1,0:T(8,128)} %copy.41) | copy-start | bytes 196612
  66.9 17.6 %copy-start.2 = (f32[256,64]{1,0:T(8,128)S(1)}, f32[256,64]{1,0:T(8,128)}, u32[]{:S(2)}) copy-start(f32[256,64]{1,0:T(8,128)} %copy.43) | copy-start | bytes 196612
  68.8 22.5 %collective-permute-start.6 = (bf16[256,1024]{1,0:T(8,128)(2,1)}, bf16[256,1024]{1,0:T(8,128)(2,1)}, u32[]{:S(2)}, u32[]{:S(2)}) collective-permute-start(bf16[256,1024]{1,0:T(8,128)(2,1)} %collective-permute-done.5), channel_id=1, source_target_pairs={{0,2},{2,4},{4,6},{6,8},{8,10},{10,12},{12,14},{1,3},{3,5},{5,7},{... | collective-permute-start | bytes 1572872 | tf_op jit(solution)/shard_map/ppermute | solution.py:23
  80.1 22.5 %collective-permute-start.3 = (bf16[256,1024]{0,1:T(8,128)(2,1)}, bf16[256,1024]{0,1:T(8,128)(2,1)S(1)}, u32[]{:S(2)}, u32[]{:S(2)}) collective-permute-start(bf16[256,1024]{0,1:T(8,128)(2,1)} %collective-permute-done.2), channel_id=1, source_target_pairs={{0,2},{2,4},{4,6},{6,8},{8,10},{10,12},{12,14},{1,3},{3,5},{5,7},{... | collective-permute-start | bytes 1572872 | tf_op jit(solution)/shard_map/ppermute | solution.py:23
  91.3 22.9 %collective-permute-start.7 = (bf16[256,1024]{1,0:T(8,128)(2,1)}, bf16[256,1024]{1,0:T(8,128)(2,1)}, u32[]{:S(2)}, u32[]{:S(2)}) collective-permute-start(bf16[256,1024]{1,0:T(8,128)(2,1)} %collective-permute-done.6), channel_id=1, source_target_pairs={{0,2},{2,4},{4,6},{6,8},{8,10},{10,12},{12,14},{1,3},{3,5},{5,7},{... | collective-permute-start | bytes 1572872 | tf_op jit(solution)/shard_map/ppermute | solution.py:23
  167.7 4.5 copy-start.9
  167.7 4.5 copy-start.13
  167.7 4.5 copy-start.17
  183.5 4.6 copy-start.9
  183.5 4.6 copy-start.13
  183.5 4.6 copy-start.17
  199.4 4.6 copy-start.9
  199.4 4.6 copy-start.13
  199.4 4.5 copy-start.17
  215.3 4.6 copy-start.9
  215.3 4.6 copy-start.13
  215.3 4.6 copy-start.17
  231.2 4.6 copy-start.9
  231.3 4.6 copy-start.13
  231.3 4.6 copy-start.17
  247.1 4.6 copy-start.9
  247.1 4.5 copy-start.13
  263.0 4.6 copy-start.9
  263.0 4.6 copy-start.13
  263.0 4.6 copy-start.17
  278.9 4.6 copy-start.9
  278.9 4.6 copy-start.13
  278.9 4.5 copy-start.17
  297.8 28.4 %collective-permute-start.14 = (f32[256,1024]{0,1:T(8,128)S(1)}, f32[256,1024]{0,1:T(8,128)S(1)}, u32[]{:S(2)}, u32[]{:S(2)}) collective-permute-start(f32[256,1024]{0,1:T(8,128)S(1)} %bitcast.238), channel_id=1, source_target_pairs={{2,0},{4,2},{6,4},{8,6},{10,8},{12,10},{14,12},{3,1},{5,3},{7,5},{... | collective-permute-start | bytes 3145736 | tf_op jit(solution)/shard_map/ppermute | solution.py:23
  299.9 48.7 %collective-permute-start.10 = (f32[256,1024]{0,1:T(8,128)S(1)}, f32[256,1024]{0,1:T(8,128)S(1)}, u32[]{:S(2)}, u32[]{:S(2)}) collective-permute-start(f32[256,1024]{0,1:T(8,128)S(1)} %bitcast.239), channel_id=1, source_target_pairs={{2,0},{4,2},{6,4},{8,6},{10,8},{12,10},{14,12},{3,1},{5,3},{7,5},{... | collective-permute-start | bytes 3145736 | tf_op jit(solution)/shard_map/ppermute | solution.py:23
  326.3 44.8 %collective-permute-start.15 = (f32[256,1024]{0,1:T(8,128)S(1)}, f32[256,1024]{0,1:T(8,128)S(1)}, u32[]{:S(2)}, u32[]{:S(2)}) collective-permute-start(f32[256,1024]{0,1:T(8,128)S(1)} %bitcast_add_fusion.3), channel_id=1, source_target_pairs={{2,0},{4,2},{6,4},{8,6},{10,8},{12,10},{14,12},{3,1},{5,3},{7,5},{... | collective-permute-start | bytes 3145736 | tf_op jit(solution)/shard_map/ppermute | solution.py:23
  348.8 44.8 %collective-permute-start.11 = (f32[256,1024]{0,1:T(8,128)S(1)}, f32[256,1024]{0,1:T(8,128)S(1)}, u32[]{:S(2)}, u32[]{:S(2)}) collective-permute-start(f32[256,1024]{0,1:T(8,128)S(1)} %bitcast_add_fusion.7), channel_id=1, source_target_pairs={{2,0},{4,2},{6,4},{8,6},{10,8},{12,10},{14,12},{3,1},{5,3},{7,5},{... | collective-permute-start | bytes 3145736 | tf_op jit(solution)/shard_map/ppermute | solution.py:23
  371.3 44.8 %collective-permute-start.16 = (f32[256,1024]{0,1:T(8,128)S(1)}, f32[256,1024]{0,1:T(8,128)S(1)}, u32[]{:S(2)}, u32[]{:S(2)}) collective-permute-start(f32[256,1024]{0,1:T(8,128)S(1)} %bitcast_add_fusion.2), channel_id=1, source_target_pairs={{2,0},{4,2},{6,4},{8,6},{10,8},{12,10},{14,12},{3,1},{5,3},{7,5},{... | collective-permute-start | bytes 3145736 | tf_op jit(solution)/shard_map/ppermute | solution.py:23
  393.7 44.8 %collective-permute-start.12 = (f32[256,1024]{0,1:T(8,128)S(1)}, f32[256,1024]{0,1:T(8,128)S(1)}, u32[]{:S(2)}, u32[]{:S(2)}) collective-permute-start(f32[256,1024]{0,1:T(8,128)S(1)} %bitcast_add_fusion.6), channel_id=1, source_target_pairs={{2,0},{4,2},{6,4},{8,6},{10,8},{12,10},{14,12},{3,1},{5,3},{7,5},{... | collective-permute-start | bytes 3145736 | tf_op jit(solution)/shard_map/ppermute | solution.py:23
  416.1 24.1 %copy-start.6 = (bf16[2,4,16,1024]{3,2,1,0:T(8,128)(2,1)S(1)}, bf16[2,4,16,1024]{3,2,1,0:T(8,128)(2,1)}, u32[]{:S(2)}) copy-start(bf16[2,4,16,1024]{3,2,1,0:T(8,128)(2,1)} %param.21) | copy-start | bytes 786436
  416.2 44.8 %collective-permute-start.17 = (f32[256,1024]{0,1:T(8,128)S(1)}, f32[256,1024]{0,1:T(8,128)S(1)}, u32[]{:S(2)}, u32[]{:S(2)}) collective-permute-start(f32[256,1024]{0,1:T(8,128)S(1)} %bitcast_add_fusion.1), channel_id=1, source_target_pairs={{2,0},{4,2},{6,4},{8,6},{10,8},{12,10},{14,12},{3,1},{5,3},{7,5},{... | collective-permute-start | bytes 3145736 | tf_op jit(solution)/shard_map/ppermute | solution.py:23
  438.7 42.0 %collective-permute-start.13 = (f32[256,1024]{0,1:T(8,128)S(1)}, f32[256,1024]{0,1:T(8,128)S(1)}, u32[]{:S(2)}, u32[]{:S(2)}) collective-permute-start(f32[256,1024]{0,1:T(8,128)S(1)} %bitcast_add_fusion.5), channel_id=1, source_target_pairs={{2,0},{4,2},{6,4},{8,6},{10,8},{12,10},{14,12},{3,1},{5,3},{7,5},{... | collective-permute-start | bytes 3145736 | tf_op jit(solution)/shard_map/ppermute | solution.py:23
  461.2 19.6 %copy-start.7 = (f32[256,64]{0,1:T(8,128)S(1)}, f32[256,64]{0,1:T(8,128)}, u32[]{:S(2)}) copy-start(f32[256,64]{0,1:T(8,128)} %get-tuple-element.290) | copy-start | bytes 196612
  490.4 3.3 collective-permute-start.8
  (38 other events, 111.6 us)
Sparse Core Ops, SparseCore 0:
  484.6 140.5 all-reduce.2
where the time goes:
time: 642 us; the launch traced here: 639 us
  waiting for transfers between devices  336 us (52%)
  matrix products  123 us (19%)
  local copies, waits for them, and re-layouts  75.9 us (12%)
  starting transfers between devices  50.3 us (8%)
  other arithmetic  39.1 us (6%)
  between operations  14.5 us (2%)
    ppermute x16, waiting for transfers between devices, passed_along_2(): lax.ppermute(value, axis, [(source, source + steps) for source in range(i...  201 us
    psum x1, waiting for transfers between devices, body(): lax.psum((down_map_gradient, up_map_gradient), ('section', 'ctx', 'dp'))  131 us
    ppermute x16, starting transfers between devices, passed_along_2(): lax.ppermute(value, axis, [(source, source + steps) for source in range(i...  50.3 us
    dot_general x16, matrix products, masked_scores(): jnp.einsum('trd,ld->trl', query_part, key_part, preferred_element_type=jn...  40.9 us
    dot_general x8, matrix products, group_backward(): jnp.einsum('trl,trd->ld', grad_scores, query_part, preferred_element_type...  31.1 us
    unnamed x52, local copies, waits for them, and re-layouts  26.1 us
    dot_general x8, matrix products, group_backward(): jnp.einsum('trl,trd->ld', weights_low, grad_part, preferred_element_type=...  24.3 us
    dot_general x8, matrix products, group_forward(): jnp.einsum('trl,ld->trd', weights, value_part, preferred_element_type=jnp...  18.2 us
  transfers between devices with their start and end apart: 19, of which 17 were waited for; matrix products, arithmetic and copies ran while one was open for 14% of the time, Pallas kernels for 0%

commit v1 on v0

--- a/solution.py
+++ b/solution.py
@@ -282,7 +282,7 @@
         value_gradient,
         adapter_up_maps,
     )
-    summed = lax.psum((down_map_gradient, up_map_gradient), ("section", "ctx", "dp"))
+    summed = lax.psum(lax.psum((down_map_gradient, up_map_gradient), ("ctx", "dp")), "section")
     return (handed, summed[0], summed[1])
 
 

time: 642 us -> 678 us (1.056)
  waiting for transfers between devices: 336 us -> 372 us
    psum x1 -> x2, waiting for transfers between devices: 131 us -> 166 us  [the longest x1 151 us: body(): lax.psum((down_map_gradient, up_map_gradient), ('ctx', 'dp'))]
  transfers between devices with their start and end apart: 19 -> 20, of which waited for: 17 -> 18; matrix products, arithmetic and copies ran while one was open for 14% -> 13% of each run, Pallas kernels for 0% -> 0%
where the time goes in v1:
time: 678 us; the launch traced here: 675 us
  waiting for transfers between devices  372 us (55%)
  matrix products  122 us (18%)
  local copies, waits for them, and re-layouts  75.9 us (11%)
  starting transfers between devices  50.2 us (7%)
  other arithmetic  39.1 us (6%)
  between operations  14.6 us (2%)
    ppermute x16, waiting for transfers between devices, passed_along_2(): lax.ppermute(value, axis, [(source, source + steps) for source in range(i...  201 us
    psum x1, waiting for transfers between devices, body(): lax.psum((down_map_gradient, up_map_gradient), ('ctx', 'dp'))  151 us
    ppermute x16, starting transfers between devices, passed_along_2(): lax.ppermute(value, axis, [(source, source + steps) for source in range(i...  50.1 us
    dot_general x16, matrix products, masked_scores(): jnp.einsum('trd,ld->trl', query_part, key_part, preferred_element_type=jn...  41 us
    dot_general x8, matrix products, group_backward(): jnp.einsum('trl,trd->ld', grad_scores, query_part, preferred_element_type...  31 us
    unnamed x52, local copies, waits for them, and re-layouts  26.1 us
    dot_general x8, matrix products, group_backward(): jnp.einsum('trl,trd->ld', weights_low, grad_part, preferred_element_type=...  24.3 us
    dot_general x8, matrix products, group_forward(): jnp.einsum('trl,ld->trd', weights, value_part, preferred_element_type=jnp...  18.2 us
  transfers between devices with their start and end apart: 20, of which 18 were waited for; matrix products, arithmetic and copies ran while one was open for 13% of the time, Pallas kernels for 0%

profile of v1, /device:TPU:0, one launch (start us, length us, event | category | flops | bytes accessed | tf_op | source)
XLA Modules:
  0.0 674.7 jit_solution(8899422376679793045)
XLA Ops:
  17.8 5.7 collective-permute-start
  24.7 3.5 collective-permute-start.4
  28.1 6.9 %collective-permute-done = bf16[256,1024]{0,1:T(8,128)(2,1)} collective-permute-done((bf16[256,1024]{0,1:T(8,128)(2,1)S(1)}, bf16[256,1024]{0,1:T(8,128)(2,1)}, u32[]{:S(2)}, u32[]{:S(2)}) %collective-permute-start) | collective-permute-done | bytes 524320 | tf_op jit(solution)/shard_map/ppermute | solution.py:23
  35.0 5.3 collective-permute-start.1
  46.4 5.2 collective-permute-start.5
  51.6 6.0 collective-permute-done.1
  57.6 5.2 collective-permute-start.2
  68.8 5.2 collective-permute-start.6
  74.1 6.0 collective-permute-done.2
  80.1 4.4 collective-permute-start.3
  87.5 3.9 collective-permute-done.6
  91.3 5.2 collective-permute-start.7
  96.5 6.1 collective-permute-done.3
  109.8 4.4 copy.48
  121.6 46.0 %while.26 = (s32[]{:T(128)}, bf16[8,256,2,128]{3,1,2,0:T(8,128)(2,1)}, f32[8,256,2]{1,2,0:T(2,128)}, bf16[8,256,2,128]{3,1,2,0:T(8,128)(2,1)}, bf16[8,1280,128]{...) while((s32[]{:T(128)}, ...), condition=%wide.region_8.9_spmd.clone, body=%wide.region_5.8_spmd.clone.sunk | while | flops 343145984 | bytes 9469813 | solution.py:245
  167.6 127.1 %while.27 = (s32[]{:T(128)}, f32[8,1280,128]{1,2,0:T(8,128)}, f32[8,1280,128]{1,2,0:T(8,128)}, bf16[8,256,2,128]{3,1,2,0:T(8,128)(2,1)}, bf16[8,1280,128]{2,1,0:...) while((s32[]{:T(128)}, f32[8,1280,128]{1,2,0:T(8,128)}, ...), condition=%wide.region_11.12_spmd.clone, body=%wide.region_9.11_spmd.clone.sunk | while | flops 678395392 | bytes 14472769 | solution.py:251
  168.9 3.3 fusion.128
  174.4 3.9 fusion.130
  184.7 3.3 fusion.128
  190.2 3.9 fusion.130
  200.7 3.3 fusion.128
  206.1 3.9 fusion.130
  212.2 3.1 fusion.131
  216.5 3.3 fusion.128
  222.0 3.9 fusion.130
  228.1 3.1 fusion.131
  232.5 3.3 fusion.128
  237.9 3.9 fusion.130
  248.3 3.3 fusion.128
  253.8 3.9 fusion.130
  259.9 3.0 fusion.131
  264.2 3.3 fusion.128
  269.6 3.9 fusion.130
  280.1 3.3 fusion.128
  285.6 3.9 fusion.130
  301.3 24.9 %collective-permute-done.14 = f32[256,1024]{0,1:T(8,128)S(1)} collective-permute-done((f32[256,1024]{0,1:T(8,128)S(1)}, f32[256,1024]{0,1:T(8,128)S(1)}, u32[]{:S(2)}, u32[]{:S(2)}) %collective-permute-start.14) | collective-permute-done | bytes 1048608 | tf_op jit(solution)/shard_map/ppermute | solution.py:23
  327.6 21.0 %collective-permute-done.10 = f32[256,1024]{0,1:T(8,128)S(1)} collective-permute-done((f32[256,1024]{0,1:T(8,128)S(1)}, f32[256,1024]{0,1:T(8,128)S(1)}, u32[]{:S(2)}, u32[]{:S(2)}) %collective-permute-start.10) | collective-permute-done | bytes 1048608 | tf_op jit(solution)/shard_map/ppermute | solution.py:23
  350.1 21.0 %collective-permute-done.15 = f32[256,1024]{0,1:T(8,128)S(1)} collective-permute-done((f32[256,1024]{0,1:T(8,128)S(1)}, f32[256,1024]{0,1:T(8,128)S(1)}, u32[]{:S(2)}, u32[]{:S(2)}) %collective-permute-start.15) | collective-permute-done | bytes 1048608 | tf_op jit(solution)/shard_map/ppermute | solution.py:23
  372.6 21.0 %collective-permute-done.11 = f32[256,1024]{0,1:T(8,128)S(1)} collective-permute-done((f32[256,1024]{0,1:T(8,128)S(1)}, f32[256,1024]{0,1:T(8,128)S(1)}, u32[]{:S(2)}, u32[]{:S(2)}) %collective-permute-start.11) | collective-permute-done | bytes 1048608 | tf_op jit(solution)/shard_map/ppermute | solution.py:23
  395.0 21.0 %collective-permute-done.16 = f32[256,1024]{0,1:T(8,128)S(1)} collective-permute-done((f32[256,1024]{0,1:T(8,128)S(1)}, f32[256,1024]{0,1:T(8,128)S(1)}, u32[]{:S(2)}, u32[]{:S(2)}) %collective-permute-start.16) | collective-permute-done | bytes 1048608 | tf_op jit(solution)/shard_map/ppermute | solution.py:23
  417.5 21.0 %collective-permute-done.12 = f32[256,1024]{0,1:T(8,128)S(1)} collective-permute-done((f32[256,1024]{0,1:T(8,128)S(1)}, f32[256,1024]{0,1:T(8,128)S(1)}, u32[]{:S(2)}, u32[]{:S(2)}) %collective-permute-start.12) | collective-permute-done | bytes 1048608 | tf_op jit(solution)/shard_map/ppermute | solution.py:23
  440.0 21.0 %collective-permute-done.17 = f32[256,1024]{0,1:T(8,128)S(1)} collective-permute-done((f32[256,1024]{0,1:T(8,128)S(1)}, f32[256,1024]{0,1:T(8,128)S(1)}, u32[]{:S(2)}, u32[]{:S(2)}) %collective-permute-start.17) | collective-permute-done | bytes 1048608 | tf_op jit(solution)/shard_map/ppermute | solution.py:23
  461.7 18.9 %collective-permute-done.13 = f32[256,1024]{0,1:T(8,128)S(1)} collective-permute-done((f32[256,1024]{0,1:T(8,128)S(1)}, f32[256,1024]{0,1:T(8,128)S(1)}, u32[]{:S(2)}, u32[]{:S(2)}) %collective-permute-start.13) | collective-permute-done | bytes 1048608 | tf_op jit(solution)/shard_map/ppermute | solution.py:23
  484.6 151.4 %all-reduce.5.cloned.1.call-done = (f32[5376,2,4,16]{0,3,2,1:T(8,128)}, f32[2,4,16,1024]{3,2,1,0:T(8,128)}) async-done(((f32[5376,2,4,16]{0,3,2,1:T(8,128)}, f32[2,4,16,1024]{3,2,1,0:T(8,128)}), (f32[5376,2,4,16]{0,3,2,1:T(8,128)}, f32[2,4,16,1024]{3,2,1,0:T(8,128)})) %all-reduce.5.cloned.1.call-update) | async-done | bytes 3276816 | tf_op jit(solution)/shard_map/psum | solution.py:285
  636.0 3.3 copy.49
  641.9 4.2 collective-permute-done.8
  646.1 15.1 %all-reduce.7.cloned.1.call-done = (f32[5376,2,4,16]{0,3,2,1:T(8,128)}, f32[2,4,16,1024]{3,2,1,0:T(8,128)}) async-done(((f32[5376,2,4,16]{0,3,2,1:T(8,128)}, f32[2,4,16,1024]{3,2,1,0:T(8,128)}), (f32[5376,2,4,16]{0,3,2,1:T(8,128)}, f32[2,4,16,1024]{3,2,1,0:T(8,128)})) %all-reduce.7.cloned.1.call-update) | async-done | bytes 3276816 | tf_op jit(solution)/shard_map/psum | solution.py:285
  663.4 3.6 copy.116
  (322 shorter events, 172.0 us)
Async XLA Ops:
  7.2 628.8 %all-reduce.5.cloned.1.call-start = ((), (), s32[]{:S(2)}) async-start(), calls=%async_computation | async-start | bytes 6553600 | tf_op jit(solution)/shard_map/psum | solution.py:285
  15.5 8.0 %copy-start.5 = (bf16[2,4,16,1024]{3,2,1,0:T(8,128)(2,1)S(1)}, bf16[2,4,16,1024]{3,2,1,0:T(8,128)(2,1)}, u32[]{:S(2)}) copy-start(bf16[2,4,16,1024]{3,2,1,0:T(8,128)(2,1)} %param.21) | copy-start | bytes 786436
  15.5 8.0 %copy-start.22 = (bf16[1,256,1024]{2,1,0:T(8,128)(2,1)S(1)}, bf16[1,256,1024]{2,1,0:T(8,128)(2,1)}, u32[]{:S(2)}) copy-start(bf16[1,256,1024]{2,1,0:T(8,128)(2,1)} %param.16) | copy-start | bytes 1572868
  17.8 17.2 %collective-permute-start = (bf16[256,1024]{0,1:T(8,128)(2,1)S(1)}, bf16[256,1024]{0,1:T(8,128)(2,1)}, u32[]{:S(2)}, u32[]{:S(2)}) collective-permute-start(bf16[256,1024]{0,1:T(8,128)(2,1)S(1)} %bitcast.243), channel_id=1, source_target_pairs={{0,2},{2,4},{4,6},{6,8},{8,10},{10,12},{12,14},{1,3},{3,5},{5,7},{... | collective-permute-start | bytes 1572872 | tf_op jit(solution)/shard_map/ppermute | solution.py:23
  24.7 21.7 %collective-permute-start.4 = (bf16[256,1024]{1,0:T(8,128)(2,1)}, bf16[256,1024]{1,0:T(8,128)(2,1)}, u32[]{:S(2)}, u32[]{:S(2)}) collective-permute-start(bf16[256,1024]{1,0:T(8,128)(2,1)} %fusion.59), channel_id=1, source_target_pairs={{0,2},{2,4},{4,6},{6,8},{8,10},{10,12},{12,14},{1,3},{3,5},{5,7},{... | collective-permute-start | bytes 1572872 | tf_op jit(solution)/shard_map/ppermute | solution.py:23
  35.0 22.6 %collective-permute-start.1 = (bf16[256,1024]{0,1:T(8,128)(2,1)}, bf16[256,1024]{0,1:T(8,128)(2,1)}, u32[]{:S(2)}, u32[]{:S(2)}) collective-permute-start(bf16[256,1024]{0,1:T(8,128)(2,1)} %collective-permute-done), channel_id=1, source_target_pairs={{0,2},{2,4},{4,6},{6,8},{8,10},{10,12},{12,14},{1,3},{3,5},{5,7},{... | collective-permute-start | bytes 1572872 | tf_op jit(solution)/shard_map/ppermute | solution.py:23
  42.6 125.1 %collective-permute-start.9 = (bf16[1,256,2048]{1,2,0:T(8,128)(2,1)}, bf16[1,256,2048]{1,2,0:T(8,128)(2,1)}, u32[]{:S(2)}, u32[]{:S(2)}) collective-permute-start(bf16[1,256,2048]{1,2,0:T(8,128)(2,1)} %copy.50), channel_id=1, source_target_pairs={{0,16},{16,0},{1,17},{17,1},{2,18},{18,2},{3,19},{19,3},{4,20},{20... | collective-permute-start | bytes 3145736 | tf_op jit(solution)/shard_map/ppermute | solution.py:17
  46.4 22.5 %collective-permute-start.5 = (bf16[256,1024]{1,0:T(8,128)(2,1)}, bf16[256,1024]{1,0:T(8,128)(2,1)}, u32[]{:S(2)}, u32[]{:S(2)}) collective-permute-start(bf16[256,1024]{1,0:T(8,128)(2,1)} %collective-permute-done.4), channel_id=1, source_target_pairs={{0,2},{2,4},{4,6},{6,8},{8,10},{10,12},{12,14},{1,3},{3,5},{5,7},{... | collective-permute-start | bytes 1572872 | tf_op jit(solution)/shard_map/ppermute | solution.py:23
  57.6 22.5 %collective-permute-start.2 = (bf16[256,1024]{0,1:T(8,128)(2,1)}, bf16[256,1024]{0,1:T(8,128)(2,1)}, u32[]{:S(2)}, u32[]{:S(2)}) collective-permute-start(bf16[256,1024]{0,1:T(8,128)(2,1)} %collective-permute-done.1), channel_id=1, source_target_pairs={{0,2},{2,4},{4,6},{6,8},{8,10},{10,12},{12,14},{1,3},{3,5},{5,7},{... | collective-permute-start | bytes 1572872 | tf_op jit(solution)/shard_map/ppermute | solution.py:23
  66.9 17.5 %copy-start.1 = (f32[256,64]{1,0:T(8,128)S(1)}, f32[256,64]{1,0:T(8,128)}, u32[]{:S(2)}) copy-start(f32[256,64]{1,0:T(8,128)} %copy.41) | copy-start | bytes 196612
  67.0 17.5 %copy-start.2 = (f32[256,64]{1,0:T(8,128)S(1)}, f32[256,64]{1,0:T(8,128)}, u32[]{:S(2)}) copy-start(f32[256,64]{1,0:T(8,128)} %copy.43) | copy-start | bytes 196612
  68.8 22.5 %collective-permute-start.6 = (bf16[256,1024]{1,0:T(8,128)(2,1)}, bf16[256,1024]{1,0:T(8,128)(2,1)}, u32[]{:S(2)}, u32[]{:S(2)}) collective-permute-start(bf16[256,1024]{1,0:T(8,128)(2,1)} %collective-permute-done.5), channel_id=1, source_target_pairs={{0,2},{2,4},{4,6},{6,8},{8,10},{10,12},{12,14},{1,3},{3,5},{5,7},{... | collective-permute-start | bytes 1572872 | tf_op jit(solution)/shard_map/ppermute | solution.py:23
  80.1 22.5 %collective-permute-start.3 = (bf16[256,1024]{0,1:T(8,128)(2,1)}, bf16[256,1024]{0,1:T(8,128)(2,1)S(1)}, u32[]{:S(2)}, u32[]{:S(2)}) collective-permute-start(bf16[256,1024]{0,1:T(8,128)(2,1)} %collective-permute-done.2), channel_id=1, source_target_pairs={{0,2},{2,4},{4,6},{6,8},{8,10},{10,12},{12,14},{1,3},{3,5},{5,7},{... | collective-permute-start | bytes 1572872 | tf_op jit(solution)/shard_map/ppermute | solution.py:23
  91.3 22.9 %collective-permute-start.7 = (bf16[256,1024]{1,0:T(8,128)(2,1)}, bf16[256,1024]{1,0:T(8,128)(2,1)}, u32[]{:S(2)}, u32[]{:S(2)}) collective-permute-start(bf16[256,1024]{1,0:T(8,128)(2,1)} %collective-permute-done.6), channel_id=1, source_target_pairs={{0,2},{2,4},{4,6},{6,8},{8,10},{10,12},{12,14},{1,3},{3,5},{5,7},{... | collective-permute-start | bytes 1572872 | tf_op jit(solution)/shard_map/ppermute | solution.py:23
  167.6 4.6 copy-start.9
  167.6 4.6 copy-start.13
  167.7 4.6 copy-start.17
  183.5 4.6 copy-start.9
  183.5 4.6 copy-start.13
  199.4 4.6 copy-start.9
  199.4 4.6 copy-start.13
  199.4 4.6 copy-start.17
  215.3 4.6 copy-start.9
  215.3 4.6 copy-start.13
  231.2 4.6 copy-start.9
  231.2 4.6 copy-start.13
  231.3 4.6 copy-start.17
  247.1 4.6 copy-start.9
  247.1 4.6 copy-start.13
  247.1 4.6 copy-start.17
  262.9 4.6 copy-start.9
  263.0 4.6 copy-start.13
  263.0 4.6 copy-start.17
  278.8 4.6 copy-start.9
  278.8 4.6 copy-start.13
  278.8 4.6 copy-start.17
  297.8 28.4 %collective-permute-start.14 = (f32[256,1024]{0,1:T(8,128)S(1)}, f32[256,1024]{0,1:T(8,128)S(1)}, u32[]{:S(2)}, u32[]{:S(2)}) collective-permute-start(f32[256,1024]{0,1:T(8,128)S(1)} %bitcast.238), channel_id=1, source_target_pairs={{2,0},{4,2},{6,4},{8,6},{10,8},{12,10},{14,12},{3,1},{5,3},{7,5},{... | collective-permute-start | bytes 3145736 | tf_op jit(solution)/shard_map/ppermute | solution.py:23
  300.0 48.7 %collective-permute-start.10 = (f32[256,1024]{0,1:T(8,128)S(1)}, f32[256,1024]{0,1:T(8,128)S(1)}, u32[]{:S(2)}, u32[]{:S(2)}) collective-permute-start(f32[256,1024]{0,1:T(8,128)S(1)} %bitcast.239), channel_id=1, source_target_pairs={{2,0},{4,2},{6,4},{8,6},{10,8},{12,10},{14,12},{3,1},{5,3},{7,5},{... | collective-permute-start | bytes 3145736 | tf_op jit(solution)/shard_map/ppermute | solution.py:23
  326.3 44.8 %collective-permute-start.15 = (f32[256,1024]{0,1:T(8,128)S(1)}, f32[256,1024]{0,1:T(8,128)S(1)}, u32[]{:S(2)}, u32[]{:S(2)}) collective-permute-start(f32[256,1024]{0,1:T(8,128)S(1)} %bitcast_add_fusion.3), channel_id=1, source_target_pairs={{2,0},{4,2},{6,4},{8,6},{10,8},{12,10},{14,12},{3,1},{5,3},{7,5},{... | collective-permute-start | bytes 3145736 | tf_op jit(solution)/shard_map/ppermute | solution.py:23
  348.8 44.8 %collective-permute-start.11 = (f32[256,1024]{0,1:T(8,128)S(1)}, f32[256,1024]{0,1:T(8,128)S(1)}, u32[]{:S(2)}, u32[]{:S(2)}) collective-permute-start(f32[256,1024]{0,1:T(8,128)S(1)} %bitcast_add_fusion.7), channel_id=1, source_target_pairs={{2,0},{4,2},{6,4},{8,6},{10,8},{12,10},{14,12},{3,1},{5,3},{7,5},{... | collective-permute-start | bytes 3145736 | tf_op jit(solution)/shard_map/ppermute | solution.py:23
  371.3 44.8 %collective-permute-start.16 = (f32[256,1024]{0,1:T(8,128)S(1)}, f32[256,1024]{0,1:T(8,128)S(1)}, u32[]{:S(2)}, u32[]{:S(2)}) collective-permute-start(f32[256,1024]{0,1:T(8,128)S(1)} %bitcast_add_fusion.2), channel_id=1, source_target_pairs={{2,0},{4,2},{6,4},{8,6},{10,8},{12,10},{14,12},{3,1},{5,3},{7,5},{... | collective-permute-start | bytes 3145736 | tf_op jit(solution)/shard_map/ppermute | solution.py:23
  393.7 44.8 %collective-permute-start.12 = (f32[256,1024]{0,1:T(8,128)S(1)}, f32[256,1024]{0,1:T(8,128)S(1)}, u32[]{:S(2)}, u32[]{:S(2)}) collective-permute-start(f32[256,1024]{0,1:T(8,128)S(1)} %bitcast_add_fusion.6), channel_id=1, source_target_pairs={{2,0},{4,2},{6,4},{8,6},{10,8},{12,10},{14,12},{3,1},{5,3},{7,5},{... | collective-permute-start | bytes 3145736 | tf_op jit(solution)/shard_map/ppermute | solution.py:23
  416.1 23.9 %copy-start.6 = (bf16[2,4,16,1024]{3,2,1,0:T(8,128)(2,1)S(1)}, bf16[2,4,16,1024]{3,2,1,0:T(8,128)(2,1)}, u32[]{:S(2)}) copy-start(bf16[2,4,16,1024]{3,2,1,0:T(8,128)(2,1)} %param.21) | copy-start | bytes 786436
  416.2 44.8 %collective-permute-start.17 = (f32[256,1024]{0,1:T(8,128)S(1)}, f32[256,1024]{0,1:T(8,128)S(1)}, u32[]{:S(2)}, u32[]{:S(2)}) collective-permute-start(f32[256,1024]{0,1:T(8,128)S(1)} %bitcast_add_fusion.1), channel_id=1, source_target_pairs={{2,0},{4,2},{6,4},{8,6},{10,8},{12,10},{14,12},{3,1},{5,3},{7,5},{... | collective-permute-start | bytes 3145736 | tf_op jit(solution)/shard_map/ppermute | solution.py:23
  438.7 42.0 %collective-permute-start.13 = (f32[256,1024]{0,1:T(8,128)S(1)}, f32[256,1024]{0,1:T(8,128)S(1)}, u32[]{:S(2)}, u32[]{:S(2)}) collective-permute-start(f32[256,1024]{0,1:T(8,128)S(1)} %bitcast_add_fusion.5), channel_id=1, source_target_pairs={{2,0},{4,2},{6,4},{8,6},{10,8},{12,10},{14,12},{3,1},{5,3},{7,5},{... | collective-permute-start | bytes 3145736 | tf_op jit(solution)/shard_map/ppermute | solution.py:23
  461.2 19.6 %copy-start.7 = (f32[256,64]{0,1:T(8,128)S(1)}, f32[256,64]{0,1:T(8,128)}, u32[]{:S(2)}) copy-start(f32[256,64]{0,1:T(8,128)} %get-tuple-element.292) | copy-start | bytes 196612
  484.5 176.6 %all-reduce.7.cloned.1.call-start = ((), (), s32[]{:S(2)}) async-start(), calls=%async_computation.1 | async-start | bytes 6553600 | tf_op jit(solution)/shard_map/psum | solution.py:285
  641.9 4.2 collective-permute-start.8
  (39 other events, 116.2 us)
Sparse Core Ops, SparseCore 0:
  484.6 151.2 all-reduce.4
  638.3 22.7 all-reduce.6
